TPU v7x, 32 devices: a whole 2x2x4 slice. The times are simulated.
32 devices in a mesh: heads: 4 (over y, x), seq: 8 (over z, core).
Axes of the slice: x: 2, y: 2, z: 4, core: 2. Of those that a mesh axis runs over, the one named last changes fastest.
Arguments:
- query: bfloat16 [24, 128, 576], P(None, 'heads'), may hold values from -1024 to 1024
- cache: bfloat16 [4096, 576], P('seq'), may hold values from -8 to 8
- segments: int32 [4096], P('seq'), may hold values from 0 to 3, as said below
- groups: int32 [24], replicated, may hold values from 0 to 3
- value_up: bfloat16 [128, 512, 128], P('heads'), may hold values from -3 to 3
- out_proj: bfloat16 [16384, 7168], P('heads', 'seq'), may hold values from -0.046875 to 0.046875
- targets: float32 [24, 7168], P(None, 'seq'), may hold values from -20 to 20
Outputs:
- projected: float32 [24, 7168], P(None, 'seq')
- loss: float32 [], replicated
- query_grad: float32 [24, 128, 576], P(None, 'heads')
- cache_grad: float32 [4096, 576], P('seq', 'heads')
Inputs may be any that keep to these rules, and one draw needn't show every extreme that they name: `segments`: constant over each aligned tile of 128 cached tokens; every group number appears in some tile.
All inputs are finite; a program needn't handle non-finite values.
Results may differ from a plain program's by a relative error of at most 0.015.
Values may be sent and summed in bfloat16 or wider, within the bound.
No kernel may reach another device: no remote copies, remote signals or barrier semaphores. Data moves between devices by JAX's collectives and lax.ppermute only.
A program may use at most 64 MiB of HBM per device.

v0:
```python
import jax
import jax.numpy as jnp
from jax import lax
from jax.sharding import PartitionSpec as P

scale_factor = 0.07216878364870322
floor_value = -1e30


def on_device(query, cache, segments, groups, value_up, out_proj, targets):
    query_len, head_count, width = query.shape
    latent = value_up.shape[1]
    vwidth = value_up.shape[2]
    row_count = query_len * head_count
    cache_len = cache.shape[0]
    query_rows = query.reshape(row_count, width)
    values = cache[:, :latent]
    allowed = groups[:, None] == segments[None, :]
    allowed_rows = jnp.broadcast_to(
        allowed[:, None, :], (query_len, head_count, cache_len)
    ).reshape(row_count, cache_len)
    scores = (
        jnp.einsum("rc,tc->rt", query_rows, cache, preferred_element_type=jnp.float32)
        * scale_factor
    )
    masked = jnp.where(allowed_rows, scores, floor_value)
    local_top = jnp.max(masked, axis=1)
    maximum = lax.pmax(local_top, "seq")
    weights = jnp.where(allowed_rows, jnp.exp(masked - maximum[:, None]), 0.0)
    totals = lax.psum(jnp.sum(weights, axis=1), "seq")
    partial_latent = jnp.dot(
        weights.astype(jnp.bfloat16), values, preferred_element_type=jnp.float32
    )
    portion = lax.psum_scatter(partial_latent, "seq", scatter_dimension=0, tiled=True)
    share_rows = portion.shape[0]
    start = lax.axis_index("seq") * share_rows
    share_totals = lax.dynamic_slice_in_dim(totals, start, share_rows)
    share_latent = (portion / share_totals[:, None]).astype(jnp.bfloat16)
    head_ids = (start + jnp.arange(share_rows, dtype=jnp.int32)) % head_count
    row_weights = jnp.take(value_up, head_ids, axis=0)
    share_value = jnp.einsum(
        "rc,rcv->rv", share_latent, row_weights, preferred_element_type=jnp.float32
    ).astype(jnp.bfloat16)
    value_out = lax.all_gather(share_value, "seq", axis=0, tiled=True).reshape(
        query_len, head_count, vwidth
    )
    flattened = value_out.reshape(query_len, head_count * vwidth)
    partial_proj = jnp.dot(flattened, out_proj, preferred_element_type=jnp.float32)
    projected = lax.psum(partial_proj, "heads")
    residual = projected - targets
    square_part = jnp.sum(residual * residual)
    model_width = targets.shape[1] * lax.axis_size("seq")
    d_projected = residual.astype(jnp.bfloat16)
    value_partial = jnp.einsum(
        "qd,rd->qr", d_projected, out_proj, preferred_element_type=jnp.float32
    )
    d_value = lax.psum(value_partial, "seq").reshape(query_len, head_count, vwidth)
    d_latent = (
        jnp.einsum(
            "qhv,hcv->qhc",
            d_value.astype(jnp.bfloat16),
            value_up,
            preferred_element_type=jnp.float32,
        )
        .astype(jnp.bfloat16)
        .reshape(row_count, latent)
    )
    row_dot = jnp.sum(d_value * value_out.astype(jnp.float32), axis=2).reshape(row_count)
    probs = weights / totals[:, None]
    d_probs = jnp.einsum("rc,tc->rt", d_latent, values, preferred_element_type=jnp.float32)
    d_scores = (scale_factor * probs * (d_probs - row_dot[:, None])).astype(jnp.bfloat16)
    query_part = jnp.dot(d_scores, cache, preferred_element_type=jnp.float32)
    square_total = lax.psum(square_part, "seq")
    query_sum = lax.psum(query_part, "seq")
    loss = square_total / (query_len * model_width)
    query_grad = query_sum.reshape(query_len, head_count, width)
    key_part = jnp.einsum("rt,rc->tc", d_scores, query_rows, preferred_element_type=jnp.float32)
    value_part = jnp.einsum(
        "rt,rc->tc", probs.astype(jnp.bfloat16), d_latent, preferred_element_type=jnp.float32
    )
    cache_part = key_part + jnp.concatenate(
        [value_part, jnp.zeros((cache_len, width - latent), jnp.float32)], axis=1
    )
    cache_grad = lax.psum_scatter(
        cache_part.astype(jnp.bfloat16), "heads", scatter_dimension=1, tiled=True
    ).astype(jnp.float32)
    return (projected, loss, query_grad, cache_grad)


def solution(mesh):
    in_specs = (
        P(None, "heads", None),
        P("seq", None),
        P("seq"),
        P(),
        P("heads", None, None),
        P("heads", "seq"),
        P(None, "seq"),
    )
    out_specs = (P(None, "seq"), P(), P(None, "heads", None), P("seq", "heads"))
    return jax.shard_map(
        on_device, mesh=mesh, in_specs=in_specs, out_specs=out_specs, check_vma=False
    )
```

profile of v0, /device:TPU:0, one launch (start us, length us, event | category | flops | bytes accessed | tf_op | source)
XLA Modules:
  0.0 309.5 jit_solution(6097966343069492329)
XLA Ops:
  8.7 2.0 fusion.25
  10.7 18.1 %pmax.7 = f32[768]{0:T(1024)S(1)} all-reduce(f32[768]{0:T(1024)S(1)} %get-tuple-element.4), channel_id=1, replica_groups=mesh['heads'=4,'seq'=8] {'seq'}, use_global_device_ids=true, to_apply=%region_1.2 | all-reduce | flops 768 | bytes 6144 | tf_op jit(solution)/shard_map/pmax | solution.py:28
  28.8 1.8 fusion.8
  31.1 13.7 %psum.35 = f32[768]{0:T(1024)S(1)} all-reduce(f32[768]{0:T(1024)S(1)} %fusion.15), channel_id=1, replica_groups=mesh['heads'=4,'seq'=8] {'seq'}, use_global_device_ids=true, to_apply=%region_4.5 | all-reduce | flops 768 | bytes 6144 | tf_op jit(solution)/shard_map/psum | solution.py:30
  45.4 8.8 %gather_fusion = bf16[96,512,128]{2,1,0:T(8,128)(2,1)} fusion(bf16[32,512,128]{2,1,0:T(8,128)(2,1)} %param.11, s32[1024]{0:T(1024)S(1)} %pad_clamp_fusion), kind=kCustom, calls=%fused_computation | custom fusion | bytes 25166208 | tf_op jit(solution)/shard_map/jit(_take)/gather | solution.py:40
  54.2 9.3 %reduce-scatter.3.cloned.1.call-done = f32[96,512]{1,0:T(8,128)} async-done(((f32[768,512]{1,0:T(8,128)}), f32[96,512]{1,0:T(8,128)}) %reduce-scatter.3.cloned.1.call-update) | async-done | bytes 196624 | tf_op jit(solution)/shard_map/reduce_scatter | solution.py:34
  63.5 1.0 fusion.16
  64.5 5.7 %fusion = f32[96,1,128]{2,1,0:T(1,128)S(1)} fusion(bf16[96,512,128]{2,1,0:T(8,128)(2,1)} %gather_fusion, pred[96]{0:T(512)(128)(4,1)S(1)} %compare_and_fusion, bf16[96,512,1]{1,0,2:T(8,128)(2,1)S(1)} %fusion.16), kind=kOutput, calls=%fused_computation.1 | convolution fusion | flops 18874368 | bytes 12730464 | tf_op jit(solution)/shard_map/rc,rcv->rv/dot_general | solution.py:41
  70.3 15.2 %all_gather.3 = bf16[768,128]{1,0:T(8,128)(2,1)} all-gather(bf16[96,128]{1,0:T(8,128)(2,1)S(1)} %convert_element_type.41), channel_id=1, replica_groups=mesh['heads'=4,'seq'=8] {'seq'}, dimensions={0}, use_global_device_ids=true | all-gather | bytes 221184 | tf_op jit(solution)/shard_map/all_gather | solution.py:44
  85.4 1.7 reshape_reshape.3
  87.1 4.9 %fusion.26 = f32[24,896]{1,0:T(8,128)} fusion(bf16[24,4096]{1,0:T(8,128)(2,1)} %reshape_reshape.3, bf16[4096,896]{1,0:T(8,128)(2,1)} %param.12), kind=kOutput, calls=%fused_computation.49 | convolution fusion | flops 176160768 | bytes 7622656 | tf_op jit(solution)/shard_map/dot_general | solution.py:48
  92.1 39.5 %all-reduce.5.cloned.1.call-done = f32[24,896]{1,0:T(8,128)} async-done(((f32[24,896]{1,0:T(8,128)}), f32[24,896]{1,0:T(8,128)}) %all-reduce.5.cloned.1.call-update) | async-done | bytes 86032 | tf_op jit(solution)/shard_map/psum | solution.py:49
  131.6 5.5 %convolution_bitcast_fusion = f32[3,32,8,128]{3,2,1,0:T(8,128)S(1)} fusion(bf16[4096,896]{1,0:T(8,128)(2,1)} %param.12, f32[24,896]{1,0:T(8,128)} %all-reduce.5.cloned.1.call-done, f32[24,896]{1,0:T(8,128)} %param.13), kind=kOutput, calls=%fused_computation.12 | convolution fusion | flops 176203776 | bytes 7905280 | tf_op jit(solution)/shard_map/qd,rd->qr/dot_general | solution.py:54
  138.0 1.7 convert.1
  139.7 54.9 %all-reduce.7.cloned.1.call-done = f32[24,32,128]{2,0,1:T(8,128)} async-done(((f32[24,32,128]{2,0,1:T(8,128)}), f32[24,32,128]{2,0,1:T(8,128)}) %all-reduce.7.cloned.1.call-update) | async-done | bytes 393232 | tf_op jit(solution)/shard_map/psum | solution.py:57
  194.6 1.4 fusion.12
  197.5 4.6 %fusion.5 = bf16[24,32,512]{2,0,1:T(8,128)(2,1)S(1)} fusion(bf16[32,512,128]{2,1,0:T(8,128)(2,1)} %param.11, f32[24,32,128]{2,0,1:T(8,128)} %all-reduce.7.cloned.1.call-done), kind=kOutput, calls=%fused_computation.11 | convolution fusion | flops 101154816 | bytes 5373952 | tf_op jit(solution)/shard_map/qhv,hcv->qhc/dot_general | solution.py:59
  205.3 1.5 fusion.4
  206.9 3.2 %fusion.27 = f32[768,576]{1,0:T(8,128)} fusion(bf16[768,512]{0,1:T(8,128)(2,1)} %copy-done.1, bf16[512,576]{0,1:T(8,128)(2,1)S(1)} %copy-done.2), kind=kOutput, calls=%fused_computation.50 | convolution fusion | flops 452984832 | bytes 3145728 | tf_op jit(solution)/shard_map/dot_general | solution.py:72
  211.6 14.3 %psum.37 = f32[]{:T(128)} all-reduce(f32[]{:T(128)} %multiply_reduce_fusion), channel_id=1, replica_groups=mesh['heads'=4,'seq'=8] {'seq'}, use_global_device_ids=true, to_apply=%region_7.8 | all-reduce | flops 1 | bytes 8 | tf_op jit(solution)/shard_map/psum | solution.py:73
  226.6 4.8 %reduce-scatter.5.cloned.1.call-done = bf16[512,144]{0,1:T(8,128)(2,1)} async-done(((bf16[512,576]{0,1:T(8,128)(2,1)}), bf16[512,144]{0,1:T(8,128)(2,1)}) %reduce-scatter.5.cloned.1.call-update) | async-done | bytes 147472 | tf_op jit(solution)/shard_map/reduce_scatter | solution.py:84
  231.4 1.7 convert_element_type.51
  233.1 65.2 %all-reduce.9.cloned.1.call-done = f32[24,32,576]{2,1,0:T(8,128)} async-done(((f32[24,32,576]{2,1,0:T(8,128)}), f32[24,32,576]{2,1,0:T(8,128)}) %all-reduce.9.cloned.1.call-update) | async-done | bytes 1769488 | tf_op jit(solution)/shard_map/psum | solution.py:74
  298.9 2.9 copy.57
  (45 shorter events, 10.3 us)
Async XLA Ops:
  7.2 1.5 copy-start
  7.2 56.3 %reduce-scatter.3.cloned.1.call-start = ((), (), s32[]{:S(2)}) async-start(), calls=%async_computation.2 | async-start | bytes 1769472 | tf_op jit(solution)/shard_map/reduce_scatter | solution.py:34
  8.7 20.1 %copy-start.2 = (bf16[512,576]{0,1:T(8,128)(2,1)S(1)}, bf16[512,576]{0,1:T(8,128)(2,1)}, u32[]{:S(2)}) copy-start(bf16[512,576]{0,1:T(8,128)(2,1)} %param.8) | copy-start | bytes 1769476
  28.8 1.9 copy-start.5
  30.6 101.0 %all-reduce.5.cloned.1.call-start = ((), (), s32[]{:S(2)}) async-start(), calls=%async_computation.3 | async-start | bytes 172032 | tf_op jit(solution)/shard_map/psum | solution.py:49
  44.8 0.6 copy-start.7
  92.0 102.6 %all-reduce.7.cloned.1.call-start = ((), (), s32[]{:S(2)}) async-start(), calls=%async_computation.4 | async-start | bytes 786432 | tf_op jit(solution)/shard_map/psum | solution.py:57
  137.9 93.5 %reduce-scatter.5.cloned.1.call-start = ((), (), s32[]{:S(2)}) async-start(), calls=%async_computation.6 | async-start | bytes 737280 | tf_op jit(solution)/shard_map/reduce_scatter | solution.py:84
  202.1 0.7 copy-start.6
  202.1 0.7 copy-start.8
  204.4 0.9 copy-start.1
  206.8 91.4 %all-reduce.9.cloned.1.call-start = ((), (), s32[]{:S(2)}) async-start(), calls=%async_computation.5 | async-start | bytes 3932160 | tf_op jit(solution)/shard_map/psum | solution.py:74
  210.1 0.9 copy-start.3
  210.1 0.9 copy-start.4
Sparse Core Ops, SparseCore 0:
  30.8 32.6 reduce-scatter.2
  92.2 39.4 all-reduce.4
  138.0 56.5 all-reduce.6
  206.9 24.4 reduce-scatter.4
  234.2 63.9 all-reduce.8
where the time goes:
time: 310 us; the launch traced here: 309 us
  waiting for transfers between devices  174 us (56%)
  blocking collectives  61.3 us (20%)
  matrix products  30.8 us (10%)
  local copies, waits for them, and re-layouts  19.9 us (6%)
  between operations  15.7 us (5%)
  other arithmetic  7.67 us (2%)
    psum x1, waiting for transfers between devices, on_device(): query_sum = lax.psum(query_part, 'seq')  65.2 us
    psum x1, waiting for transfers between devices, on_device(): lax.psum(value_partial, 'seq').reshape(query_len, head_count, vwidth)  54.9 us
    psum x1, waiting for transfers between devices, on_device(): projected = lax.psum(partial_proj, 'heads')  39.5 us
    pmax x1, blocking collectives, on_device(): maximum = lax.pmax(local_top, 'seq')  18.1 us
    all_gather x1, blocking collectives, on_device(): lax.all_gather(share_value, 'seq', axis=0, tiled=True)  15.2 us
    psum x1, blocking collectives, on_device(): square_total = lax.psum(square_part, 'seq')  14.3 us
    psum x1, blocking collectives, on_device(): totals = lax.psum(jnp.sum(weights, axis=1), 'seq')  13.7 us
    reduce_scatter x1, waiting for transfers between devices, on_device(): lax.psum_scatter(partial_latent, 'seq', scatter_dimension=0, tiled=True)  9.28 us
  transfers between devices with their start and end apart: 5, of which 5 were waited for; matrix products, arithmetic and copies ran while one was open for 5% of the time, Pallas kernels for 0%

commit v1 on v0

--- a/solution.py
+++ b/solution.py
@@ -71,7 +71,7 @@
     d_scores = (scale_factor * probs * (d_probs - row_dot[:, None])).astype(jnp.bfloat16)
     query_part = jnp.dot(d_scores, cache, preferred_element_type=jnp.float32)
     square_total = lax.psum(square_part, "seq")
-    query_sum = lax.psum(query_part, "seq")
+    query_sum = jnp.sum(lax.all_gather(query_part, "seq"), axis=0)
     loss = square_total / (query_len * model_width)
     query_grad = query_sum.reshape(query_len, head_count, width)
     key_part = jnp.einsum("rt,rc->tc", d_scores, query_rows, preferred_element_type=jnp.float32)

time: 310 us -> 400 us (1.29)
  waiting for transfers between devices: 174 us -> 239 us
  local copies, waits for them, and re-layouts: 19.9 us -> 34.6 us
  other arithmetic: 7.67 us -> 15 us
    all_gather x0 -> x1, waiting for transfers between devices: none -> 130 us  [on_device(): query_sum = jnp.sum(lax.all_gather(query_part, 'seq'), axis=0)]
    psum x1 -> x0, waiting for transfers between devices: 65.2 us -> none  [on_device(): query_sum = lax.psum(query_part, 'seq')]
    unnamed x20 -> x24, local copies, waits for them, and re-layouts: 6.34 us -> 19.2 us
    reduce_sum x0 -> x1, other arithmetic: none -> 8.39 us  [on_device(): query_sum = jnp.sum(lax.all_gather(query_part, 'seq'), axis=0)]
  transfers between devices with their start and end apart: 5 -> 5, of which waited for: 5 -> 5; matrix products, arithmetic and copies ran while one was open for 5% -> 4% of each run, Pallas kernels for 0% -> 0%
where the time goes in v1:
time: 400 us; the launch traced here: 399 us
  waiting for transfers between devices  239 us (60%)
  blocking collectives  61.3 us (15%)
  local copies, waits for them, and re-layouts  34.6 us (9%)
  matrix products  32.8 us (8%)
  between operations  15.7 us (4%)
  other arithmetic  15 us (4%)
    all_gather x1, waiting for transfers between devices, on_device(): query_sum = jnp.sum(lax.all_gather(query_part, 'seq'), axis=0)  130 us
    psum x1, waiting for transfers between devices, on_device(): lax.psum(value_partial, 'seq').reshape(query_len, head_count, vwidth)  54.9 us
    psum x1, waiting for transfers between devices, on_device(): projected = lax.psum(partial_proj, 'heads')  39.6 us
    unnamed x24, local copies, waits for them, and re-layouts  19.2 us
    pmax x1, blocking collectives, on_device(): maximum = lax.pmax(local_top, 'seq')  18.1 us
    all_gather x1, blocking collectives, on_device(): lax.all_gather(share_value, 'seq', axis=0, tiled=True)  15.2 us
    psum x1, blocking collectives, on_device(): square_total = lax.psum(square_part, 'seq')  14.3 us
    psum x1, blocking collectives, on_device(): totals = lax.psum(jnp.sum(weights, axis=1), 'seq')  13.7 us
  transfers between devices with their start and end apart: 5, of which 5 were waited for; matrix products, arithmetic and copies ran while one was open for 4% of the time, Pallas kernels for 0%

profile of v1, /device:TPU:0, one launch (start us, length us, event | category | flops | bytes accessed | tf_op | source)
XLA Modules:
  0.0 399.0 jit_solution(9553835041896644769)
XLA Ops:
  8.7 2.0 fusion.25
  10.7 18.1 %pmax.7 = f32[768]{0:T(1024)S(1)} all-reduce(f32[768]{0:T(1024)S(1)} %get-tuple-element.8), channel_id=1, replica_groups=mesh['heads'=4,'seq'=8] {'seq'}, use_global_device_ids=true, to_apply=%region_1.2 | all-reduce | flops 768 | bytes 6144 | tf_op jit(solution)/shard_map/pmax | solution.py:28
  28.8 1.8 fusion.8
  31.1 13.7 %psum.28 = f32[768]{0:T(1024)S(1)} all-reduce(f32[768]{0:T(1024)S(1)} %fusion.15), channel_id=1, replica_groups=mesh['heads'=4,'seq'=8] {'seq'}, use_global_device_ids=true, to_apply=%region_4.5 | all-reduce | flops 768 | bytes 6144 | tf_op jit(solution)/shard_map/psum | solution.py:30
  44.9 8.8 %gather_fusion = bf16[96,512,128]{2,1,0:T(8,128)(2,1)} fusion(bf16[32,512,128]{2,1,0:T(8,128)(2,1)} %param.11, s32[1024]{0:T(1024)S(1)} %pad_clamp_fusion), kind=kCustom, calls=%fused_computation | custom fusion | bytes 25166208 | tf_op jit(solution)/shard_map/jit(_take)/gather | solution.py:40
  53.7 9.7 %reduce-scatter.3.cloned.1.call-done = f32[96,512]{1,0:T(8,128)} async-done(((f32[768,512]{1,0:T(8,128)}), f32[96,512]{1,0:T(8,128)}) %reduce-scatter.3.cloned.1.call-update) | async-done | bytes 196624 | tf_op jit(solution)/shard_map/reduce_scatter | solution.py:34
  64.4 5.8 %fusion = f32[96,1,128]{2,1,0:T(1,128)S(1)} fusion(bf16[96,512,128]{2,1,0:T(8,128)(2,1)} %gather_fusion, pred[96]{0:T(512)(128)(4,1)S(1)} %compare_and_fusion, bf16[96,512,1]{1,0,2:T(8,128)(2,1)S(1)} %fusion.16), kind=kOutput, calls=%fused_computation.2 | convolution fusion | flops 18874368 | bytes 12730464 | tf_op jit(solution)/shard_map/rc,rcv->rv/dot_general | solution.py:41
  70.2 15.2 %all_gather.9 = bf16[768,128]{1,0:T(8,128)(2,1)} all-gather(bf16[96,128]{1,0:T(8,128)(2,1)S(1)} %convert_element_type.41), channel_id=1, replica_groups=mesh['heads'=4,'seq'=8] {'seq'}, dimensions={0}, use_global_device_ids=true | all-gather | bytes 221184 | tf_op jit(solution)/shard_map/all_gather | solution.py:44
  85.3 1.7 reshape_reshape.3
  87.0 4.9 %fusion.26 = f32[24,896]{1,0:T(8,128)} fusion(bf16[24,4096]{1,0:T(8,128)(2,1)} %reshape_reshape.3, bf16[4096,896]{1,0:T(8,128)(2,1)} %param.12), kind=kOutput, calls=%fused_computation.50 | convolution fusion | flops 176160768 | bytes 7622656 | tf_op jit(solution)/shard_map/dot_general | solution.py:48
  92.0 39.6 %all-reduce.4.cloned.1.call-done = f32[24,896]{1,0:T(8,128)} async-done(((f32[24,896]{1,0:T(8,128)}), f32[24,896]{1,0:T(8,128)}) %all-reduce.4.cloned.1.call-update) | async-done | bytes 86032 | tf_op jit(solution)/shard_map/psum | solution.py:49
  131.6 5.5 %convolution_bitcast_fusion = f32[3,32,8,128]{3,2,1,0:T(8,128)S(1)} fusion(bf16[4096,896]{1,0:T(8,128)(2,1)} %param.12, f32[24,896]{1,0:T(8,128)} %all-reduce.4.cloned.1.call-done, f32[24,896]{1,0:T(8,128)} %param.13), kind=kOutput, calls=%fused_computation.13 | convolution fusion | flops 176203776 | bytes 7905280 | tf_op jit(solution)/shard_map/qd,rd->qr/dot_general | solution.py:54
  137.9 1.7 convert.1
  139.7 54.9 %all-reduce.6.cloned.1.call-done = f32[24,32,128]{2,0,1:T(8,128)} async-done(((f32[24,32,128]{2,0,1:T(8,128)}), f32[24,32,128]{2,0,1:T(8,128)}) %all-reduce.6.cloned.1.call-update) | async-done | bytes 393232 | tf_op jit(solution)/shard_map/psum | solution.py:57
  194.6 4.6 %fusion.5 = bf16[24,32,512]{2,0,1:T(8,128)(2,1)S(1)} fusion(bf16[32,512,128]{2,1,0:T(8,128)(2,1)} %param.11, f32[24,32,128]{2,0,1:T(8,128)} %all-reduce.6.cloned.1.call-done), kind=kOutput, calls=%fused_computation.12 | convolution fusion | flops 101154816 | bytes 5373952 | tf_op jit(solution)/shard_map/qhv,hcv->qhc/dot_general | solution.py:59
  199.5 1.7 fusion.6
  203.0 2.1 multiply_convert_fusion
  207.7 3.0 fusion.27
  212.2 14.3 %psum.30 = f32[]{:T(128)} all-reduce(f32[]{:T(128)} %multiply_reduce_fusion), channel_id=1, replica_groups=mesh['heads'=4,'seq'=8] {'seq'}, use_global_device_ids=true, to_apply=%region_7.8 | all-reduce | flops 1 | bytes 8 | tf_op jit(solution)/shard_map/psum | solution.py:73
  227.2 4.9 %reduce-scatter.5.cloned.1.call-done = bf16[512,144]{0,1:T(8,128)(2,1)} async-done(((bf16[512,576]{0,1:T(8,128)(2,1)}), bf16[512,144]{0,1:T(8,128)(2,1)}) %reduce-scatter.5.cloned.1.call-update) | async-done | bytes 147472 | tf_op jit(solution)/shard_map/reduce_scatter | solution.py:84
  233.8 130.0 %all-gather.3.cloned.1.call-done = f32[6144,576]{0,1:T(8,128)} async-done(((f32[768,576]{0,1:T(8,128)}), f32[6144,576]{0,1:T(8,128)}) %all-gather.3.cloned.1.call-update) | async-done | bytes 14155792 | tf_op jit(solution)/shard_map/all_gather | solution.py:74
  363.8 16.8 %copy.38 = f32[72,8,8,768]{3,2,1,0:T(8,128)} copy(f32[72,8,8,768]{3,1,2,0:T(8,128)} %bitcast.38) | data formatting | bytes 28311552
  380.6 8.4 %bitcast_reduce_fusion = f32[768,576]{0,1:T(8,128)S(1)} fusion(f32[72,8,8,768]{3,2,1,0:T(8,128)} %copy.38), kind=kLoop, calls=%fused_computation.1 | loop fusion | flops 3096576 | bytes 15925248 | tf_op jit(solution)/shard_map/reduce_sum | solution.py:74
  389.0 1.8 copy.33
  (51 shorter events, 12.4 us)
Async XLA Ops:
  7.2 1.5 copy-start
  7.2 56.2 %reduce-scatter.3.cloned.1.call-start = ((), (), s32[]{:S(2)}) async-start(), calls=%async_computation.2 | async-start | bytes 1769472 | tf_op jit(solution)/shard_map/reduce_scatter | solution.py:34
  8.7 20.1 %copy-start.2 = (bf16[512,576]{0,1:T(8,128)(2,1)S(1)}, bf16[512,576]{0,1:T(8,128)(2,1)}, u32[]{:S(2)}) copy-start(bf16[512,576]{0,1:T(8,128)(2,1)} %param.8) | copy-start | bytes 1769476
  28.8 170.6 %copy-start.9 = (f32[768]{0:T(1024)}, f32[768]{0:T(1024)S(1)}, u32[]{:S(2)}) copy-start(f32[768]{0:T(1024)S(1)} %pmax.7) | copy-start | bytes 9220
  30.6 101.0 %all-reduce.4.cloned.1.call-start = ((), (), s32[]{:S(2)}) async-start(), calls=%async_computation.3 | async-start | bytes 172032 | tf_op jit(solution)/shard_map/psum | solution.py:49
  44.8 154.7 %copy-start.10 = (f32[768]{0:T(1024)}, f32[768]{0:T(1024)S(1)}, u32[]{:S(2)}) copy-start(f32[768]{0:T(1024)S(1)} %psum.28) | copy-start | bytes 9220
  92.0 102.6 %all-reduce.6.cloned.1.call-start = ((), (), s32[]{:S(2)}) async-start(), calls=%async_computation.4 | async-start | bytes 786432 | tf_op jit(solution)/shard_map/psum | solution.py:57
  137.9 94.2 %reduce-scatter.5.cloned.1.call-start = ((), (), s32[]{:S(2)}) async-start(), calls=%async_computation.5 | async-start | bytes 737280 | tf_op jit(solution)/shard_map/reduce_scatter | solution.py:84
  199.4 1.8 copy-start.6
  199.5 1.8 copy-start.3
  199.5 1.7 copy-start.4
  203.0 3.0 copy-start.5
  205.1 0.9 copy-start.1
  207.5 156.3 %all-gather.3.cloned.1.call-start = ((), (), s32[]{:S(2)}) async-start(), calls=%async_computation.6 | async-start | bytes 15925248 | tf_op jit(solution)/shard_map/all_gather | solution.py:74
  210.7 0.9 copy-start.7
  210.7 0.9 copy-start.8
Sparse Core Ops, SparseCore 0:
  30.8 32.5 reduce-scatter.2
  92.1 39.4 all-reduce.3
  138.0 56.5 all-reduce.5
  207.6 24.4 reduce-scatter.4
  234.1 129.5 all-gather.2
